TPU v7x, 32 devices: a 4x2x2 block of a 4x4x8 slice. The times are simulated.
32 devices in a mesh: dp: 4 (over y, z), tp: 8 (over x, core).
Axes of the slice: x: 4, y: 2, z: 2, core: 2. Of those that a mesh axis runs over, the one named last changes fastest.
The devices are a block of a 4x4x8 slice.
Arguments:
- ids: int32 [8, 256], P('dp'), parts along dimension 0
- E: bfloat16 [32768, 2048], P('tp')
- g: bfloat16 [2048], replicated
- W: bfloat16 [2048, 3072], P(None, 'tp')
- du: bfloat16 [8, 256, 3072], P('dp', None, 'tp'), parts along dimension 0
- dres: bfloat16 [8, 256, 2048], P('dp', 'tp'), parts along dimension 0
Outputs:
- output 1: bfloat16 [8, 256, 3072], P('dp', None, 'tp'), parts along dimension 0
- output 2: bfloat16 [8, 256, 2048], P('dp', 'tp'), parts along dimension 0
- output 3: float32 [131072, 2048], P(('dp', 'tp')), parts along dimension 0
- output 4: float32 [8192, 3072], P('dp', 'tp'), parts along dimension 0
- output 5: float32 [8192], P('dp'), parts along dimension 0
There are 4 independent parts. A program takes and returns all parts, laid end to end along the dimension named above; an argument that names none is the same for every part.
All inputs are finite; a program needn't handle non-finite values.
Results may differ from a plain program's by a relative error of at most 0.00675624.
Values are sent between devices in bfloat16 or wider.
A program may use at most 768 MiB of HBM per device.

v0:
```python
import jax
import jax.numpy as jnp
from jax import lax
from jax.sharding import PartitionSpec as P

EPS = 1e-6


def solution(mesh):
    ntp = mesh.shape["tp"]

    def body(ids, E, g, W, du, dres):
        vs, d = E.shape
        nk, t = ids.shape
        ts = t // ntp
        me = lax.axis_index("tp")
        lo = me * vs
        gf = g.astype(jnp.float32)
        rows = lax.broadcasted_iota(jnp.int32, (vs, t), 0)
        c0 = (((0,), (0,)), ((), ()))
        c1 = (((1,), (1,)), ((), ()))
        dE = None
        dW = None
        dg = jnp.zeros((d,), jnp.float32)
        us = []
        xs = []
        for k in range(nk):
            oh = (rows == (ids[k] - lo)[None, :]).astype(jnp.bfloat16)
            xp = lax.dot_general(oh, E, c0, preferred_element_type=jnp.float32).astype(jnp.bfloat16)
            x = lax.psum(xp, "tp")
            xf = x.astype(jnp.float32)
            rs = lax.rsqrt(jnp.mean(xf * xf, axis=-1, keepdims=True) + EPS)
            nh = xf * rs
            n = (nh * gf).astype(jnp.bfloat16)
            us.append(jnp.dot(n, W, preferred_element_type=jnp.float32).astype(jnp.bfloat16))
            xs.append(lax.dynamic_slice_in_dim(x, me * ts, ts, 0))
            p = lax.dot_general(du[k], W, c1, preferred_element_type=jnp.float32).astype(jnp.bfloat16)
            got = lax.all_to_all(p.reshape(ntp, ts, d), "tp", 0, 0, tiled=True)
            dn = jnp.sum(got.astype(jnp.float32), axis=0)
            nhl = lax.dynamic_slice_in_dim(nh, me * ts, ts, 0)
            rsl = lax.dynamic_slice_in_dim(rs, me * ts, ts, 0)
            gdn = gf * dn
            dx = dres[k].astype(jnp.float32) + rsl * (gdn - nhl * jnp.mean(nhl * gdn, axis=-1, keepdims=True))
            dg = dg + jnp.sum(dn * nhl, axis=0)
            dxa = lax.all_gather(dx.astype(jnp.bfloat16), "tp", axis=0, tiled=True)
            de = jnp.dot(oh, dxa, preferred_element_type=jnp.float32)
            dE = de if dE is None else dE + de
            dw = lax.dot_general(n, du[k], c0, preferred_element_type=jnp.float32)
            dW = dw if dW is None else dW + dw
        dg = lax.psum(dg, "tp")
        return jnp.stack(us), jnp.stack(xs), dE, dW, dg

    return jax.shard_map(
        body,
        mesh=mesh,
        in_specs=(P("dp", None), P("tp", None), P(None), P(None, "tp"), P("dp", None, "tp"), P("dp", "tp", None)),
        out_specs=(P("dp", None, "tp"), P("dp", "tp", None), P(("dp", "tp"), None), P("dp", "tp"), P("dp")),
        check_vma=False,
    )
```

profile of v0, /device:TPU:81, one launch (start us, length us, event | category | flops | bytes accessed | tf_op | source)
XLA Modules:
  0.0 189.7 jit_solution(8026492915498523363)
XLA Ops:
  7.2 1.4 copy-done
  8.6 2.6 %convolution_convert_fusion = bf16[256,2048]{1,0:T(8,128)(2,1)} fusion(bf16[2048,384]{1,0:T(8,128)(2,1)S(1)} %copy-done, bf16[2,256,384]{2,1,0:T(8,128)(2,1)} %param.10), kind=kOutput, calls=%fused_computation.13 | convolution fusion | flops 403177472 | bytes 2818048 | tf_op jit(solution)/shard_map/dot_general | solution.py:37
  11.2 6.1 %all-to-all-start.1 = ((bf16[8,32,2048]{2,1,0:T(8,128)(2,1)}), bf16[8,32,2048]{2,1,0:T(8,128)(2,1)S(1)}, u32[]{:S(2)}, u32[]{:S(2)}) async-start(bf16[8,32,2048]{2,1,0:T(8,128)(2,1)} %bitcast.37), calls=%async_computation.1 | async-start | bytes 2097152 | tf_op jit(solution)/shard_map/all_to_all | solution.py:38
  17.4 1.8 convolution_convert_fusion.1
  19.2 9.3 %fusion.3 = bf16[256,2048]{1,0:T(8,128)(2,1)} fusion(bf16[4096,2048]{1,0:T(8,128)(2,1)} %param.7, s32[256]{0:T(256)S(1)} %bitcast.38), kind=kOutput, calls=%fused_computation.11 | convolution fusion | flops 4296540160 | bytes 17826816 | tf_op jit(solution)/shard_map/dot_general | solution.py:29
  28.5 3.6 %all-to-all-done.1 = bf16[8,32,2048]{2,1,0:T(8,128)(2,1)S(1)} async-done(((bf16[8,32,2048]{2,1,0:T(8,128)(2,1)}), bf16[8,32,2048]{2,1,0:T(8,128)(2,1)S(1)}, u32[]{:S(2)}, u32[]{:S(2)}) %all-to-all-start.1) | async-done | bytes 1048608 | tf_op jit(solution)/shard_map/all_to_all | solution.py:38
  32.1 5.3 %all-to-all-start = ((bf16[8,32,2048]{2,1,0:T(8,128)(2,1)}), bf16[8,32,2048]{2,1,0:T(8,128)(2,1)}, u32[]{:S(2)}, u32[]{:S(2)}) async-start(bf16[8,32,2048]{2,1,0:T(8,128)(2,1)} %bitcast.36), calls=%async_computation | async-start | bytes 2097152 | tf_op jit(solution)/shard_map/all_to_all | solution.py:38
  37.5 9.3 %fusion.4 = bf16[256,2048]{1,0:T(8,128)(2,1)} fusion(bf16[4096,2048]{1,0:T(8,128)(2,1)} %param.7, s32[256]{0:T(256)S(1)} %bitcast.40), kind=kOutput, calls=%fused_computation.12 | convolution fusion | flops 4296540160 | bytes 17826816 | tf_op jit(solution)/shard_map/dot_general | solution.py:29
  46.9 0.5 copy-done.16
  47.5 0.1 convert_reduce_fusion
  47.6 4.8 %all-to-all-done = bf16[8,32,2048]{2,1,0:T(8,128)(2,1)} async-done(((bf16[8,32,2048]{2,1,0:T(8,128)(2,1)}), bf16[8,32,2048]{2,1,0:T(8,128)(2,1)}, u32[]{:S(2)}, u32[]{:S(2)}) %all-to-all-start) | async-done | bytes 1048608 | tf_op jit(solution)/shard_map/all_to_all | solution.py:38
  52.4 1.4 convert_reduce_fusion.1
  53.8 53.7 %all-reduce.3.cloned.1.call-done = (bf16[256,2048]{1,0:T(8,128)(2,1)}, bf16[256,2048]{1,0:T(8,128)(2,1)}) async-done(((bf16[256,2048]{1,0:T(8,128)(2,1)}, bf16[256,2048]{1,0:T(8,128)(2,1)}), (bf16[256,2048]{1,0:T(8,128)(2,1)}, bf16[256,2048]{1,0:T(8,128)(2,1)})) %all-reduce.3.cloned.1.call-update) | async-done | bytes 2097168 | tf_op jit(solution)/shard_map/psum | solution.py:30
  107.5 1.7 fusion.6
  109.2 1.5 fusion.5
  110.8 0.3 convert_multiply_fusion
  111.1 0.2 copy-done.12
  111.3 0.1 dynamic-slice.6
  111.4 0.1 dynamic-slice.7
  111.5 0.7 multiply_reduce_fusion
  112.2 0.9 fusion.14
  113.2 0.7 add.62
  113.9 16.0 %psum.23 = f32[2048]{0:T(1024)} all-reduce(f32[2048]{0:T(1024)S(1)} %add.62), channel_id=1, replica_groups=mesh['dp'=4,'tp'=8] {'tp'}, use_global_device_ids=true, to_apply=%region_10.0 | all-reduce | flops 2048 | bytes 16384 | tf_op jit(solution)/shard_map/psum | solution.py:50
  129.9 0.9 dynamic-slice_bitcast_fusion
  130.9 2.0 %fusion.11 = bf16[1,256,384]{2,1,0:T(8,128)(2,1)S(1)} fusion(bf16[2048,384]{1,0:T(8,128)(2,1)S(1)} %copy-done, f32[2048]{0:T(1024)S(1)} %convert_element_type.61, bf16[256,2048]{1,0:T(8,128)(2,1)} %get-tuple-element.10, f32[256]{0:T(256)} %copy-done.12), kind=kOutput, calls=%fused_computation.27 | convolution fusion | flops 404848640 | bytes 2827264 | tf_op jit(solution)/shard_map/dot_general | solution.py:35
  132.9 1.4 fusion.12
  134.4 2.5 %fusion.13 = f32[2048,384]{1,0:T(8,128)} fusion(f32[2048]{0:T(1024)S(1)} %convert_element_type.61, bf16[2,256,384]{2,1,0:T(8,128)(2,1)S(1)} %copy-done.5, bf16[256,2048]{1,0:T(8,128)(2,1)S(1)} %copy-done.4, f32[256]{0:T(256)S(1)} %copy-done.13), kind=kOutput, calls=%fused_computation.29 | convolution fusion | flops 404750336 | bytes 4400128 | tf_op jit(solution)/shard_map/dot_general | solution.py:48
  136.9 0.7 pad_maximum_fusion.1
  137.7 0.8 pad_maximum_fusion
  138.5 4.4 %convolution_add_fusion.1 = f32[2048,384]{1,0:T(8,128)} fusion(f32[2048,384]{1,0:T(8,128)} %fusion.13, f32[2048]{0:T(1024)S(1)} %convert_element_type.61, bf16[2,256,384]{2,1,0:T(8,128)(2,1)S(1)} %copy-done.5, bf16[256,2048]{1,0:T(8,128)(2,1)S(1)} %copy-done.2, f32[256]{0:T(256)S(1)} %copy-done.11), kind=kOutput, calls=%fused_computation.6 | convolution fusion | flops 405536768 | bytes 7545856 | tf_op jit(solution)/shard_map/dot_general | solution.py:48
  142.9 15.3 %fusion.1 = f32[4096,2048]{1,0:T(8,128)} fusion(bf16[256,2048]{1,0:T(8,128)(2,1)} %all-gather.3.cloned.1.call-done, s32[256]{0:T(256)S(1)} %bitcast.39), kind=kOutput, calls=%fused_computation.4 | convolution fusion | flops 4296015872 | bytes 34604032 | tf_op jit(solution)/shard_map/dot_general | solution.py:46
  158.2 24.9 %convolution_add_fusion = f32[4096,2048]{1,0:T(8,128)} fusion(f32[4096,2048]{1,0:T(8,128)} %fusion.1, bf16[256,2048]{1,0:T(8,128)(2,1)} %all-gather.5.cloned.1.call-done, s32[256]{0:T(256)S(1)} %bitcast.41), kind=kOutput, calls=%fused_computation | convolution fusion | flops 4304404480 | bytes 68158464 | tf_op jit(solution)/shard_map/dot_general | solution.py:46
  (47 shorter events, 0.4 us)
Async XLA Ops:
  7.2 1.4 copy-start
  7.2 10.2 %copy-start.5 = (bf16[2,256,384]{2,1,0:T(8,128)(2,1)S(1)}, bf16[2,256,384]{2,1,0:T(8,128)(2,1)}, u32[]{:S(2)}) copy-start(bf16[2,256,384]{2,1,0:T(8,128)(2,1)} %param.10) | copy-start | bytes 1179652
  11.2 7.9 %copy-start.17 = (s32[2,256]{1,0:T(2,128)S(1)}, s32[2,256]{1,0:T(2,128)}, u32[]{:S(2)}) copy-start(s32[2,256]{1,0:T(2,128)} %param.6) | copy-start | bytes 6148
  11.2 20.9 %all-to-all-start.1 = ((bf16[8,32,2048]{2,1,0:T(8,128)(2,1)}), bf16[8,32,2048]{2,1,0:T(8,128)(2,1)S(1)}, u32[]{:S(2)}, u32[]{:S(2)}) async-start(bf16[8,32,2048]{2,1,0:T(8,128)(2,1)} %bitcast.37), calls=%async_computation.1 | async-start | bytes 2097152 | tf_op jit(solution)/shard_map/all_to_all | solution.py:38
  19.2 9.3 %copy-start.8 = (s32[1,256]{1,0:T(1,128)}, s32[1,256]{1,0:T(1,128)S(1)}, u32[]{:S(2)}) copy-start(s32[1,256]{1,0:T(1,128)S(1)} %get-tuple-element.15) | copy-start | bytes 3076
  19.2 18.3 %copy-start.14 = (s32[1,256]{1,0:T(1,128)}, s32[1,256]{1,0:T(1,128)S(1)}, u32[]{:S(2)}) copy-start(s32[1,256]{1,0:T(1,128)S(1)} %get-tuple-element.16) | copy-start | bytes 3076
  32.1 20.3 %all-to-all-start = ((bf16[8,32,2048]{2,1,0:T(8,128)(2,1)}), bf16[8,32,2048]{2,1,0:T(8,128)(2,1)}, u32[]{:S(2)}, u32[]{:S(2)}) async-start(bf16[8,32,2048]{2,1,0:T(8,128)(2,1)} %bitcast.36), calls=%async_computation | async-start | bytes 2097152 | tf_op jit(solution)/shard_map/all_to_all | solution.py:38
  37.5 70.1 %all-reduce.3.cloned.1.call-start = ((), (), s32[]{:S(2)}) async-start(), calls=%async_computation.4 | async-start | bytes 4194304 | tf_op jit(solution)/shard_map/psum | solution.py:30
  46.8 0.7 copy-start.16
  46.9 96.1 %all-gather.3.cloned.1.call-start = ((), (), s32[]{:S(2)}) async-start(), calls=%async_computation.2 | async-start | bytes 1179648 | tf_op jit(solution)/shard_map/all_gather | solution.py:45
  107.5 3.2 %copy-start.2 = (bf16[256,2048]{1,0:T(8,128)(2,1)S(1)}, bf16[256,2048]{1,0:T(8,128)(2,1)}, u32[]{:S(2)}) copy-start(bf16[256,2048]{1,0:T(8,128)(2,1)} %get-tuple-element.9) | copy-start | bytes 3145732
  107.5 3.2 %copy-start.3 = (bf16[256,2048]{1,0:T(8,128)(2,1)S(1)}, bf16[256,2048]{1,0:T(8,128)(2,1)}, u32[]{:S(2)}) copy-start(bf16[256,2048]{1,0:T(8,128)(2,1)} %get-tuple-element.10) | copy-start | bytes 3145732
  109.2 2.2 %copy-start.10 = (f32[256]{0:T(256)}, f32[256]{0:T(256)S(1)}, u32[]{:S(2)}) copy-start(f32[256]{0:T(256)S(1)} %add_rsqrt_fusion) | copy-start | bytes 3076
  110.8 0.6 copy-start.12
  110.8 1.5 copy-start.6
  113.2 45.0 %all-gather.5.cloned.1.call-start = ((), (), s32[]{:S(2)}) async-start(), calls=%async_computation.3 | async-start | bytes 1179648 | tf_op jit(solution)/shard_map/all_gather | solution.py:45
  129.9 3.0 %copy-start.11 = (f32[256]{0:T(256)S(1)}, f32[256]{0:T(256)}, u32[]{:S(2)}) copy-start(f32[256]{0:T(256)} %copy-done.10) | copy-start | bytes 3076
  132.9 1.5 copy-start.4
  132.9 1.5 copy-start.13
  134.4 3.3 %copy-start.7 = (bf16[1,256,384]{2,1,0:T(8,128)(2,1)S(1)}, bf16[1,256,384]{2,1,0:T(8,128)(2,1)}, u32[]{:S(2)}) copy-start(bf16[1,256,384]{2,1,0:T(8,128)(2,1)} %fusion.12) | copy-start | bytes 589828
  138.5 4.4 %copy-start.9 = (s32[1,256]{1,0:T(1,128)S(1)}, s32[1,256]{1,0:T(1,128)}, u32[]{:S(2)}) copy-start(s32[1,256]{1,0:T(1,128)} %copy-done.8) | copy-start | bytes 3076
  142.9 15.3 %copy-start.15 = (s32[1,256]{1,0:T(1,128)S(1)}, s32[1,256]{1,0:T(1,128)}, u32[]{:S(2)}) copy-start(s32[1,256]{1,0:T(1,128)} %copy-done.14) | copy-start | bytes 3076
  158.2 24.9 %copy-start.1 = (bf16[2048,384]{1,0:T(8,128)(2,1)S(1)}, bf16[2048,384]{1,0:T(8,128)(2,1)}, u32[]{:S(2)}) copy-start(bf16[2048,384]{1,0:T(8,128)(2,1)} %param.9) | copy-start | bytes 4718596
Sparse Core Ops, SparseCore 0:
  47.0 60.5 all-reduce.2
  113.3 21.8 all-gather.2
  137.1 19.7 all-gather.4
where the time goes:
time: 190 us
  matrix products  73.6 us (39%)
  waiting for transfers between devices  62.3 us (33%)
  blocking collectives  16 us (8%)
  between operations  13.9 us (7%)
  starting transfers between devices  11.6 us (6%)
  other arithmetic  8.92 us (5%)
  local copies, waits for them, and re-layouts  3.28 us (2%)
    psum x1, waiting for transfers between devices, body(): x = lax.psum(xp, 'tp')  53.7 us
    dot_general x2, matrix products, body(): de = jnp.dot(oh, dxa, preferred_element_type=jnp.float32)  40.2 us
    dot_general x2, matrix products, body(): lax.dot_general(oh, E, c0, preferred_element_type=jnp.float32)  18.6 us
    psum x1, blocking collectives, body(): dg = lax.psum(dg, 'tp')  16 us
    all_to_all x2, starting transfers between devices, body(): got = lax.all_to_all(p.reshape(ntp, ts, d), 'tp', 0, 0, tiled=True)  11.5 us
    all_to_all x2, waiting for transfers between devices, body(): got = lax.all_to_all(p.reshape(ntp, ts, d), 'tp', 0, 0, tiled=True)  8.44 us
    dot_general x2, matrix products, body(): dw = lax.dot_general(n, du[k], c0, preferred_element_type=jnp.float32)  6.94 us
    dot_general x2, matrix products, body(): lax.dot_general(du[k], W, c1, preferred_element_type=jnp.float32)  4.4 us
  transfers between devices with their start and end apart: 5, of which 3 were waited for; matrix products, arithmetic and copies ran while one was open for 27% of the time, Pallas kernels for 0%

commit v1 on v0

v1 whole, which is shorter than its diff:
```python
import jax
import jax.numpy as jnp
from jax import lax
from jax.experimental import pallas as pl
from jax.experimental.pallas import tpu as pltpu
from jax.sharding import PartitionSpec as P

EPS = 1e-6
F32 = jnp.float32
BF16 = jnp.bfloat16
MESH = pl.DeviceIdType.MESH

PX, P1, P2, P3 = 0, 1, 3, 5
XX, X1, X2, X3 = 7, 8, 10, 12
AGX, AGD, DG, NSEM = 14, 28, 42, 49
A1, A2, A3, B0, B1, B2, B3 = 0, 2, 4, 6, 8, 10, 12


def comm_kernel(ids_ref, e_ref, g_ref, w_ref, du_ref, dres_ref,
                n_ref, dx_ref, x_ref, dg_ref,
                ev, acc, idc, p, pin, s, r1, fin, xp, xin, xr1, xfin, xfull, dxfull, dgall,
                esem, ssem, rsem):
    nk, ntp, ts, d = xfull.shape
    nchip = ntp // 2
    t = nk * ntp * ts
    ne, er, _ = ev.shape
    me = lax.axis_index("tp")
    c, k = me // 2, me % 2
    partner = 2 * c + 1 - k
    chips = [(c + 1) % nchip, (c + nchip - 1) % nchip]
    opp = (c + 2) % nchip
    nbr = [2 * q + k for q in chips]

    def rcopy(i, src, dst, to):
        return pltpu.make_async_remote_copy(
            src_ref=src, dst_ref=dst, send_sem=ssem.at[i], recv_sem=rsem.at[i],
            device_id={"tp": to}, device_id_type=MESH)

    def ecopy(i):
        return pltpu.make_async_copy(e_ref.at[i], ev.at[i], esem.at[i])

    barrier = pltpu.get_barrier_semaphore()
    for j in range(1, ntp):
        pl.semaphore_signal(barrier, inc=1, device_id={"tp": (me + j) % ntp}, device_id_type=MESH)
    for i in range(ne):
        ecopy(i).start()

    nt = 256

    @pl.loop(0, d // nt)
    def _(j):
        cols = pl.ds(pl.multiple_of(j * nt, nt), nt)
        o = lax.dot_general(du_ref[...], w_ref[cols, :], (((1,), (1,)), ((), ())),
                            preferred_element_type=F32).astype(BF16)
        p[:, :, :, :, cols] = o.reshape(nk, nchip, 2, ts, nt)

    pl.semaphore_wait(barrier, ntp - 1)
    cpx = rcopy(PX, p.at[:, :, 1 - k], pin, partner)
    cpx.start()

    for h in range(nk):
        row = jnp.broadcast_to(ids_ref[h:h + 1, :], (128, ntp * ts))
        idc[h * ntp * ts:(h + 1) * ntp * ts, :] = jnp.transpose(row)

    cpx.wait_recv()

    def pair(h, q):
        return p[h, q, k].astype(F32) + pin[h, q].astype(F32)

    sends = []
    for dr in range(2):
        s[dr, opp] = pair(dr, opp)
        cp = rcopy(P1 + dr, s.at[dr, opp], r1.at[dr], nbr[dr])
        cp.start()
        sends.append(cp)
    for dr in range(2):
        s[1 - dr, chips[dr]] = pair(1 - dr, chips[dr])
        cp = rcopy(P2 + dr, s.at[1 - dr, chips[dr]], fin.at[dr, 1 - dr], nbr[dr])
        cp.start()
        sends.append(cp)

    lo = me * (ne * er)
    lane = lax.broadcasted_iota(jnp.int32, (t, er), 1)
    acc[...] = jnp.zeros_like(acc)
    nc = 512

    @pl.loop(0, ne)
    def _(i):
        ecopy(i).wait()
        idv = idc[...] - (lo + i * er)
        oh = (jnp.concatenate([idv] * (er // 128), axis=1) == lane).astype(BF16)

        @pl.loop(0, d // nc)
        def _(j):
            cols = pl.ds(pl.multiple_of(j * nc, nc), nc)
            acc[:, cols] += jnp.dot(oh, ev[i, :, cols], preferred_element_type=F32)

    xp[...] = acc[...].astype(BF16).reshape(xp.shape)
    cxx = rcopy(XX, xp.at[:, :, 1 - k], xin, partner)
    cxx.start()
    cxx.wait_recv()

    def xpair(h, q):
        return (xp[h, q, k].astype(F32) + xin[h, q].astype(F32)).astype(BF16)

    cxx.wait_send()
    for dr in range(2):
        xp[dr, opp, k] = xpair(dr, opp)
        cp = rcopy(X1 + dr, xp.at[dr, opp, k], xr1.at[dr], nbr[dr])
        cp.start()
        sends.append(cp)
    for dr in range(2):
        xp[1 - dr, chips[dr], k] = xpair(1 - dr, chips[dr])
        cp = rcopy(X2 + dr, xp.at[1 - dr, chips[dr], k], xfin.at[dr, 1 - dr], nbr[dr])
        cp.start()
        sends.append(cp)
    for dr in range(2):
        v = xpair(dr, chips[dr]).astype(F32)
        rcopy(X1 + dr, xp.at[dr, opp, k], xr1.at[dr], nbr[dr]).wait_recv()
        xp[dr, chips[dr], k] = (v + xr1[dr].astype(F32)).astype(BF16)
        cp = rcopy(X3 + dr, xp.at[dr, chips[dr], k], xfin.at[dr, dr], nbr[dr])
        cp.start()
        sends.append(cp)
    for dr in range(2):
        rcopy(P1 + dr, s.at[dr, opp], r1.at[dr], nbr[dr]).wait_recv()
        s[dr, chips[dr]] = pair(dr, chips[dr]) + r1[dr]
        cp = rcopy(P3 + dr, s.at[dr, chips[dr]], fin.at[dr, dr], nbr[dr])
        cp.start()
        sends.append(cp)

    def ag_start(base, full):
        for dr in range(2):
            for m, h in ((A1, dr), (A2, 1 - dr)):
                cp = rcopy(base + m + dr, full.at[h, me], full.at[h, me], nbr[dr])
                cp.start()
                sends.append(cp)
        for h in range(2):
            cp = rcopy(base + B0 + h, full.at[h, me], full.at[h, me], partner)
            cp.start()
            sends.append(cp)

    def ag_recv(base, full, m, b, dr, h, owner, forward):
        blk = full.at[h, owner]
        rcopy(base + m + dr, blk, blk, nbr[dr]).wait_recv()
        if forward:
            cp = rcopy(base + A3 + dr, blk, blk, nbr[dr])
            cp.start()
            sends.append(cp)
        cp = rcopy(base + b + dr, blk, blk, partner)
        cp.start()
        sends.append(cp)

    def ag_near(base, full):
        for dr in range(2):
            ag_recv(base, full, A1, B1, dr, dr, nbr[1 - dr], True)
        for dr in range(2):
            ag_recv(base, full, A2, B2, dr, 1 - dr, nbr[1 - dr], False)

    def ag_far(base, full):
        for dr in range(2):
            ag_recv(base, full, A3, B3, dr, dr, 2 * opp + k, False)

    def ag_end(base, full):
        for b in (B0, B1, B2, B3):
            for i in range(2):
                blk = full.at[0, 0]
                rcopy(base + b + i, blk, blk, partner).wait_recv()

    for h in range(nk):
        v = xpair(h, c).astype(F32)
        for dr in range(2):
            m = X3 if h == dr else X2
            rcopy(m + dr, xfin.at[dr, h], xfin.at[dr, h], nbr[dr]).wait_recv()
            v = v + xfin[dr, h].astype(F32)
        v = v.astype(BF16)
        xfull[h, me] = v
        x_ref[h] = v
    ag_start(AGX, xfull)

    gf = g_ref[...].astype(F32)
    dgp = jnp.zeros((1, d), F32)
    for h in range(nk):
        xf = x_ref[h].astype(F32)
        rs = lax.rsqrt(jnp.mean(xf * xf, axis=-1, keepdims=True) + EPS)
        nh = xf * rs
        dn = pair(h, c)
        for dr in range(2):
            m = P3 if h == dr else P2
            rcopy(m + dr, fin.at[dr, h], fin.at[dr, h], nbr[dr]).wait_recv()
            dn = dn + fin[dr, h]
        gdn = gf * dn
        dxv = dres_ref[h].astype(F32) + rs * (gdn - nh * jnp.mean(nh * gdn, axis=-1, keepdims=True))
        dgp = dgp + jnp.sum(dn * nh, axis=0, keepdims=True)
        dxfull[h, me] = dxv.astype(BF16)
    ag_start(AGD, dxfull)
    dgall[me] = dgp
    for j in range(1, ntp):
        cp = rcopy(DG + j - 1, dgall.at[me], dgall.at[me], (me + j) % ntp)
        cp.start()
        sends.append(cp)

    ag_near(AGX, xfull)
    ag_near(AGD, dxfull)
    ag_far(AGX, xfull)
    ag_end(AGX, xfull)

    @pl.loop(0, nk * ntp)
    def _(i):
        h, q = i // ntp, i % ntp
        xf = xfull[h, q].astype(F32)
        rs = lax.rsqrt(jnp.mean(xf * xf, axis=-1, keepdims=True) + EPS)
        n_ref[h, q] = (xf * rs * gf).astype(BF16)

    for j in range(1, ntp):
        rcopy(DG + j - 1, dgall.at[me], dgall.at[me], (me + j) % ntp).wait_recv()
    tot = dgall[0]
    for j in range(1, ntp):
        tot = tot + dgall[j]
    dg_ref[...] = tot

    ag_far(AGD, dxfull)
    ag_end(AGD, dxfull)
    dx_ref[...] = dxfull[...]
    cpx.wait_send()
    for cp in sends:
        cp.wait_send()


def out_kernel(ids_ref, dx_ref, n_ref, nt_ref, du_ref, w_ref, x_ref, dg_ref,
               de_ref, dw_ref, u_ref, xo_ref, dgo_ref):
    i = pl.program_id(0)
    rows = de_ref.shape[0]
    nk, t = ids_ref.shape
    me = lax.axis_index("tp")
    lo = me * (rows * pl.num_programs(0)) + i * rows
    sub = lax.broadcasted_iota(jnp.int32, (rows, t), 0) + lo
    oh = jnp.concatenate([(ids_ref[h:h + 1, :] == sub).astype(BF16) for h in range(nk)], axis=1)
    de_ref[...] = jnp.dot(oh, dx_ref[...], preferred_element_type=F32)
    dw_ref[...] = lax.dot_general(nt_ref[...], du_ref[...], (((0,), (0,)), ((), ())),
                                  preferred_element_type=F32)

    @pl.when(i == 0)
    def _():
        xo_ref[...] = x_ref[...]
        dgo_ref[...] = dg_ref[...]

    @pl.when(i < nk)
    def _():
        r = pl.ds(pl.multiple_of(i * t, t), t)
        u_ref[...] = jnp.dot(n_ref[r, :], w_ref[...], preferred_element_type=F32).astype(BF16)


def solution(mesh):
    ntp = mesh.shape["tp"]

    def body(ids, E, g, W, du, dres):
        vs, d = E.shape
        nk, t = ids.shape
        ts = t // ntp
        fs = W.shape[1]
        nchip = ntp // 2
        er = 512
        ne = vs // er
        g2 = g.reshape(1, d)
        du2 = du.reshape(nk * t, fs)
        vm = pl.BlockSpec(memory_space=pltpu.VMEM)
        hb = pl.BlockSpec(memory_space=pl.ANY)
        n, dxa, x, dg = pl.pallas_call(
            comm_kernel,
            out_shape=(
                jax.ShapeDtypeStruct((nk, ntp, ts, d), BF16),
                jax.ShapeDtypeStruct((nk, ntp, ts, d), BF16),
                jax.ShapeDtypeStruct((nk, ts, d), BF16),
                jax.ShapeDtypeStruct((1, d), F32),
            ),
            in_specs=[vm, hb, vm, vm, vm, vm],
            out_specs=(vm, vm, vm, vm),
            scratch_shapes=[
                pltpu.VMEM((ne, er, d), BF16),
                pltpu.VMEM((nk * t, d), F32),
                pltpu.VMEM((nk * t, 128), jnp.int32),
                pltpu.VMEM((nk, nchip, 2, ts, d), BF16),
                pltpu.VMEM((nk, nchip, ts, d), BF16),
                pltpu.VMEM((nk, nchip, ts, d), F32),
                pltpu.VMEM((2, ts, d), F32),
                pltpu.VMEM((2, nk, ts, d), F32),
                pltpu.VMEM((nk, nchip, 2, ts, d), BF16),
                pltpu.VMEM((nk, nchip, ts, d), BF16),
                pltpu.VMEM((2, ts, d), BF16),
                pltpu.VMEM((2, nk, ts, d), BF16),
                pltpu.VMEM((nk, ntp, ts, d), BF16),
                pltpu.VMEM((nk, ntp, ts, d), BF16),
                pltpu.VMEM((ntp, 1, d), F32),
                pltpu.SemaphoreType.DMA((ne,)),
                pltpu.SemaphoreType.DMA((NSEM,)),
                pltpu.SemaphoreType.DMA((NSEM,)),
            ],
            compiler_params=pltpu.CompilerParams(
                collective_id=0, has_side_effects=True, vmem_limit_bytes=60 << 20),
            name="comm",
        )(ids, E.reshape(ne, er, d), g2, W, du2, dres)
        n2 = n.reshape(nk * t, d)
        rt = 256
        ng = vs // rt
        full = lambda *sh: pl.BlockSpec(sh, lambda i: (0,) * len(sh))
        dE, dW, u, xo, dgo = pl.pallas_call(
            out_kernel,
            grid=(ng,),
            out_shape=(
                jax.ShapeDtypeStruct((vs, d), F32),
                jax.ShapeDtypeStruct((d, fs), F32),
                jax.ShapeDtypeStruct((nk * t, fs), BF16),
                jax.ShapeDtypeStruct((nk, ts, d), BF16),
                jax.ShapeDtypeStruct((1, d), F32),
            ),
            in_specs=[
                full(nk, t), full(nk * t, d), full(nk * t, d),
                pl.BlockSpec((nk * t, d // ng), lambda i: (0, i)),
                full(nk * t, fs), full(d, fs), full(nk, ts, d), full(1, d),
            ],
            out_specs=(
                pl.BlockSpec((rt, d), lambda i: (i, 0)),
                pl.BlockSpec((d // ng, fs), lambda i: (i, 0)),
                pl.BlockSpec((t, fs), lambda i: (jnp.minimum(i, nk - 1), 0)),
                full(nk, ts, d), full(1, d),
            ),
            compiler_params=pltpu.CompilerParams(vmem_limit_bytes=48 << 20),
            name="outs",
        )(ids, dxa.reshape(nk * t, d), n2, n2, du2, W, x, dg)
        return u.reshape(nk, t, fs), xo, dE, dW, dgo.reshape(d)

    return jax.shard_map(
        body,
        mesh=mesh,
        in_specs=(P("dp", None), P("tp", None), P(None), P(None, "tp"), P("dp", None, "tp"), P("dp", "tp", None)),
        out_specs=(P("dp", None, "tp"), P("dp", "tp", None), P(("dp", "tp"), None), P("dp", "tp"), P("dp")),
        check_vma=False,
    )
```

time: 190 us -> 94.2 us (0.50)
  Pallas kernels: 0 us -> 88.5 us
  matrix products: 73.6 us -> 0 us
  waiting for transfers between devices: 62.3 us -> 0 us
  blocking collectives: 16 us -> 0 us
  between operations: 13.9 us -> 0.68 us
  starting transfers between devices: 11.6 us -> 0 us
  other arithmetic: 8.92 us -> 0 us
    pallas_call x0 -> x2, Pallas kernels: none -> 88.5 us  [the longest x1 67.1 us: body(): pl.pallas_call(comm_kernel, out_shape=(jax.ShapeDtypeStruct((nk, ntp, ts,...]
    dot_general x10 -> x0, matrix products: 73.6 us -> none  [the longest x2 40.2 us: body(): de = jnp.dot(oh, dxa, preferred_element_type=jnp.float32)]
    psum x1 -> x0, waiting for transfers between devices: 53.7 us -> none  [body(): x = lax.psum(xp, 'tp')]
    psum x1 -> x0, blocking collectives: 16 us -> none  [body(): dg = lax.psum(dg, 'tp')]
    all_to_all x2 -> x0, starting transfers between devices: 11.5 us -> none  [body(): got = lax.all_to_all(p.reshape(ntp, ts, d), 'tp', 0, 0, tiled=True)]
    all_to_all x2 -> x0, waiting for transfers between devices: 8.44 us -> none  [body(): got = lax.all_to_all(p.reshape(ntp, ts, d), 'tp', 0, 0, tiled=True)]
    reduce_sum x5 -> x0, other arithmetic: 5.45 us -> none  [the longest x2 3.17 us: body(): rs = lax.rsqrt(jnp.mean(xf * xf, axis=-1, keepdims=True) + EPS)]
  transfers between devices with their start and end apart: 5 -> 0, of which waited for: 3 -> 0; matrix products, arithmetic and copies ran while one was open for 27% -> 0% of each run, Pallas kernels for 0% -> 0%
where the time goes in v1:
time: 94.2 us; the launch traced here: 93.7 us
  Pallas kernels  88.5 us (94%)
  local copies, waits for them, and re-layouts  4.53 us (5%)
    pallas_call x1, Pallas kernels, body(): pl.pallas_call(comm_kernel, out_shape=(jax.ShapeDtypeStruct((nk, ntp, ts,...  67.1 us
    pallas_call x1, Pallas kernels, body(): pl.pallas_call(out_kernel, grid=(ng,), out_shape=(jax.ShapeDtypeStruct((v...  21.4 us
    unnamed x12, local copies, waits for them, and re-layouts  3.24 us

profile of v1, /device:TPU:81, one launch (start us, length us, event | category | flops | bytes accessed | tf_op | source)
XLA Modules:
  0.0 93.7 jit_solution(17331960650634103513)
XLA Ops:
  0.6 1.3 %reshape.32.g_ref = bf16[1,2048]{1,0:T(2,128)(2,1)} reshape(bf16[2048]{0:T(1024)(128)(2,1)} %param.8) | data formatting | bytes 8192 | tf_op jit(solution)/shard_map/reshape | solution.py:264
  1.9 0.0 copy-start
  1.9 0.0 copy-start.2
  1.9 0.0 copy-start.5
  1.9 67.1 %comm.1 = (bf16[2,8,32,2048]{3,2,1,0:T(8,128)(2,1)}, bf16[2,8,32,2048]{3,2,1,0:T(8,128)(2,1)}, bf16[2,32,2048]{2,1,0:T(8,128)(2,1)}, f32[1,2048]{1,0:T(1,128)}) custom-call(s32[2,256]{1,0:T(2,128)} %ids_ref.3, bf16[8,512,2048]{2,1,0:T(8,128)(2,1)} %bitcast.9, bf16[1,2048]{1,0:T(2,128)(2,1)} %reshape.32.g_ref, bf16[2048,384]{1,0:T(8,128)(2,1)} %w_ref.3, ...), custom_call_target="tpu_custom_call" | custom-call | tf_op jit(solution)/shard_map/comm/pallas_call | solution.py:268
  69.1 0.0 copy-done
  69.1 0.0 copy-done.2
  69.1 0.0 copy-done.5
  69.1 0.0 copy-start.1
  69.1 1.6 %copy-done.1 = bf16[2,8,32,2048]{3,2,1,0:T(8,128)(2,1)S(1)} copy-done((bf16[2,8,32,2048]{3,2,1,0:T(8,128)(2,1)S(1)}, bf16[2,8,32,2048]{3,2,1,0:T(8,128)(2,1)}, u32[]{:S(2)}) %copy-start.1) | copy-done | bytes 2097176
  70.7 0.0 copy-start.3
  70.7 0.9 %copy-done.3 = bf16[2,32,2048]{2,1,0:T(8,128)(2,1)S(1)} copy-done((bf16[2,32,2048]{2,1,0:T(8,128)(2,1)S(1)}, bf16[2,32,2048]{2,1,0:T(8,128)(2,1)}, u32[]{:S(2)}) %copy-start.3) | copy-done | bytes 262168
  71.6 0.0 copy-start.4
  71.6 0.7 copy-done.4
  72.3 21.4 %outs.1 = (f32[4096,2048]{1,0:T(8,128)}, f32[2048,384]{1,0:T(8,128)}, bf16[512,384]{1,0:T(8,128)(2,1)}, bf16[2,32,2048]{2,1,0:T(8,128)(2,1)}, f32[1,2048]{1,0:T(1,128)}) custom-call(s32[2,256]{1,0:T(2,128)S(1)} %copy-done.5, bf16[512,2048]{1,0:T(8,128)(2,1)S(1)} %bitcast.6, bf16[512,2048]{1,0:T(8,128)(2,1)} %bitcast.10, bf16[512,2048]{1,0:T(8,128)(2,1)} %bitcast.11, ...), custom_call_target="tpu_custom_call" | custom-call | tf_op jit(solution)/shard_map/outs/pallas_call | solution.py:306
Async XLA Ops:
  1.9 67.1 %copy-start = (bf16[2048,384]{1,0:T(8,128)(2,1)S(1)}, bf16[2048,384]{1,0:T(8,128)(2,1)}, u32[]{:S(2)}) copy-start(bf16[2048,384]{1,0:T(8,128)(2,1)} %w_ref.3) | copy-start | bytes 4718596
  1.9 67.1 %copy-start.2 = (bf16[2,256,384]{2,1,0:T(8,128)(2,1)S(1)}, bf16[2,256,384]{2,1,0:T(8,128)(2,1)}, u32[]{:S(2)}) copy-start(bf16[2,256,384]{2,1,0:T(8,128)(2,1)} %param.10) | copy-start | bytes 1179652
  1.9 67.2 %copy-start.5 = (s32[2,256]{1,0:T(2,128)S(1)}, s32[2,256]{1,0:T(2,128)}, u32[]{:S(2)}) copy-start(s32[2,256]{1,0:T(2,128)} %ids_ref.3) | copy-start | bytes 6148
  69.1 1.6 %copy-start.1 = (bf16[2,8,32,2048]{3,2,1,0:T(8,128)(2,1)S(1)}, bf16[2,8,32,2048]{3,2,1,0:T(8,128)(2,1)}, u32[]{:S(2)}) copy-start(bf16[2,8,32,2048]{3,2,1,0:T(8,128)(2,1)} %get-tuple-element.14) | copy-start | bytes 6291460
  70.7 0.9 %copy-start.3 = (bf16[2,32,2048]{2,1,0:T(8,128)(2,1)S(1)}, bf16[2,32,2048]{2,1,0:T(8,128)(2,1)}, u32[]{:S(2)}) copy-start(bf16[2,32,2048]{2,1,0:T(8,128)(2,1)} %get-tuple-element.16.x_ref) | copy-start | bytes 786436
  71.6 0.7 copy-start.4
